TPU v7x, 32 devices: a whole 2x2x4 slice. The times are simulated.
32 devices in a mesh: dp: 4 (over x, core), section: 4 (over z), tensor: 2 (over y).
Axes of the slice: x: 2, y: 2, z: 4, core: 2. Of those that a mesh axis runs over, the one named last changes fastest.
Arguments:
- weight_gate: bfloat16 [4096, 11008], P(None, ('dp', 'tensor')), may hold values from -0.09375 to 0.09375
- weight_up: bfloat16 [4096, 11008], P(None, ('dp', 'tensor')), may hold values from -0.09375 to 0.09375
- weight_down: bfloat16 [11008, 4096], P(('dp', 'tensor')), may hold values from -0.0546875 to 0.0546875
- acts_in: bfloat16 [4, 64, 4096], P('section', ('dp', 'tensor')), may hold values from -6 to 6
- grads_in: bfloat16 [4, 64, 4096], P('section', ('dp', 'tensor')), may hold values from -6 to 6
- saved_acts: bfloat16 [4, 4, 64, 4096], P('section', None, ('dp', 'tensor')), may hold values from -6 to 6
- saved_grads: bfloat16 [4, 4, 64, 4096], P('section', None, ('dp', 'tensor')), may hold values from -6 to 6
- plan: int32 [4, 2], P('section'), may hold values from 0 to 3
Outputs:
- next_acts: bfloat16 [4, 64, 4096], P('section', ('dp', 'tensor'))
- next_grads: bfloat16 [4, 64, 4096], P('section', ('dp', 'tensor'))
- grad_gate: bfloat16 [4, 4096, 11008], P('section', None, ('dp', 'tensor'))
- grad_up: bfloat16 [4, 4096, 11008], P('section', None, ('dp', 'tensor'))
All inputs are finite; a program needn't handle non-finite values.
Results may differ from a plain program's by a relative error of at most 0.0085.
Values may be sent and summed in bfloat16 or wider, within the bound.
A program may use at most 128 MiB of HBM per device.

v0:
```python
import jax
import jax.numpy as jnp
from jax import lax
from jax.sharding import PartitionSpec as P

EPS = 0.5


def shifted(block, axis, distance):
    devices = range(lax.axis_size(axis))
    route = [(i - distance, i) for i in devices if i - distance in devices]
    return lax.ppermute(block, axis, route)


def rms_scale(row_block):
    mean_sq = jnp.mean(row_block * row_block, axis=-1, keepdims=True)
    return row_block * lax.rsqrt(mean_sq + EPS)


def gated(normed, w_gate, w_up):
    gate_pre = jnp.dot(normed, w_gate, preferred_element_type=jnp.float32)
    up_pre = jnp.dot(normed, w_up, preferred_element_type=jnp.float32)
    return (gate_pre, up_pre)


def back_gates(cotangent, w_down, gate_pre, up_pre):
    d_act = lax.dot_general(
        cotangent, w_down, (((1,), (1,)), ((), ())), preferred_element_type=jnp.float32
    )
    sigmoid_gate = jax.nn.sigmoid(gate_pre)
    d_up = (d_act * gate_pre * sigmoid_gate).astype(jnp.bfloat16)
    d_gate = (d_act * up_pre * sigmoid_gate * (1.0 + gate_pre * (1.0 - sigmoid_gate))).astype(
        jnp.bfloat16
    )
    return (d_gate, d_up)


def contract_rows(left, right):
    return lax.dot_general(
        left, right, (((0,), (0,)), ((), ())), preferred_element_type=jnp.float32
    )


def body(weight_gate, weight_up, weight_down, acts_in, grads_in, saved_acts, saved_grads, plan):
    front_rows = acts_in[0]
    cot_back = grads_in[0]
    back_rows = lax.dynamic_index_in_dim(saved_acts[0], plan[0, 0], 0, keepdims=False)
    late_rows = lax.dynamic_index_in_dim(saved_acts[0], plan[0, 1], 0, keepdims=False)
    cot_late = lax.dynamic_index_in_dim(saved_grads[0], plan[0, 1], 0, keepdims=False)
    norm_front = rms_scale(front_rows.astype(jnp.float32)).astype(jnp.bfloat16)
    norm_back = rms_scale(back_rows.astype(jnp.float32)).astype(jnp.bfloat16)
    norm_late = rms_scale(late_rows.astype(jnp.float32)).astype(jnp.bfloat16)
    in_group = (
        lax.all_gather(norm_front, "tensor", axis=0, tiled=True),
        lax.all_gather(norm_back, "tensor", axis=0, tiled=True),
        lax.all_gather(cot_back, "tensor", axis=0, tiled=True),
        lax.all_gather(norm_late, "tensor", axis=0, tiled=True),
        lax.all_gather(cot_late, "tensor", axis=0, tiled=True),
    )
    gathered = (
        lax.all_gather(in_group[0], "dp", axis=0, tiled=True),
        lax.all_gather(in_group[1], "dp", axis=0, tiled=True),
        lax.all_gather(in_group[2], "dp", axis=0, tiled=True),
        lax.all_gather(in_group[3], "dp", axis=0, tiled=True),
        lax.all_gather(in_group[4], "dp", axis=0, tiled=True),
    )
    all_front, all_back, all_cot_back, all_late, all_cot_late = gathered
    gate_front, up_front = gated(all_front, weight_gate, weight_up)
    act_front = (jax.nn.silu(gate_front) * up_front).astype(jnp.bfloat16)
    gate_back, up_back = gated(all_back, weight_gate, weight_up)
    dgate_back, dup_back = back_gates(all_cot_back, weight_down, gate_back, up_back)
    branch = jnp.dot(act_front, weight_down, preferred_element_type=jnp.float32)
    d_norm = lax.dot_general(
        dgate_back, weight_gate, (((1,), (1,)), ((), ())), preferred_element_type=jnp.float32
    )
    d_norm = d_norm + lax.dot_general(
        dup_back, weight_up, (((1,), (1,)), ((), ())), preferred_element_type=jnp.float32
    )
    dp_block = lax.psum_scatter(
        jnp.concatenate([branch, d_norm], axis=1).astype(jnp.bfloat16),
        "dp",
        scatter_dimension=0,
        tiled=True,
    )
    summed = lax.psum_scatter(dp_block, "tensor", scatter_dimension=0, tiled=True).astype(
        jnp.float32
    )
    model_width = front_rows.shape[1]
    branch_rows = summed[:, :model_width]
    d_norm_rows = summed[:, model_width:]
    out_front = (front_rows.astype(jnp.float32) + branch_rows).astype(jnp.bfloat16)
    unused, norm_pull = jax.vjp(rms_scale, back_rows.astype(jnp.float32))
    d_input = norm_pull(d_norm_rows)[0]
    d_rows = (cot_back.astype(jnp.float32) + d_input).astype(jnp.bfloat16)
    next_acts = shifted(out_front, "section", 1)
    next_grads = shifted(d_rows, "section", -1)
    gate_late, up_late = gated(all_late, weight_gate, weight_up)
    dgate_late, dup_late = back_gates(all_cot_late, weight_down, gate_late, up_late)
    grad_gate = contract_rows(all_late, dgate_late).astype(jnp.bfloat16)
    grad_up = contract_rows(all_late, dup_late).astype(jnp.bfloat16)
    return (next_acts[None], next_grads[None], grad_gate[None], grad_up[None])


def solution(mesh):
    placed = (
        P(None, ("dp", "tensor")),
        P(None, ("dp", "tensor")),
        P(("dp", "tensor"), None),
        P("section", ("dp", "tensor"), None),
        P("section", ("dp", "tensor"), None),
        P("section", None, ("dp", "tensor"), None),
        P("section", None, ("dp", "tensor"), None),
        P("section", None),
    )
    return jax.shard_map(
        body,
        mesh=mesh,
        in_specs=placed,
        out_specs=(
            P("section", ("dp", "tensor"), None),
            P("section", ("dp", "tensor"), None),
            P("section", None, ("dp", "tensor")),
            P("section", None, ("dp", "tensor")),
        ),
        check_vma=False,
    )
```

profile of v0, /device:TPU:0, one launch (start us, length us, event | category | flops | bytes accessed | tf_op | source)
XLA Modules:
  0.0 205.4 jit_solution(18396390760276424230)
XLA Ops:
  7.2 0.0 copy-start
  7.2 0.0 reduce-scatter.3.cloned.1.call-start
  7.2 1.0 fusion.31
  8.3 1.3 fusion.43
  11.5 0.0 copy-start.1
  11.5 1.1 fusion.34
  12.7 1.2 fusion.32
  13.9 6.0 %all_gather.30 = bf16[16,4096]{1,0:T(8,128)(2,1)S(1)} all-gather(bf16[8,4096]{1,0:T(8,128)(2,1)S(1)} %fusion.32), channel_id=1, replica_groups=mesh['dp'=4,'section'=4,'tensor'=2] {'tensor'}, dimensions={0}, use_global_device_ids=true | all-gather | bytes 196608 | tf_op jit(solution)/shard_map/all_gather | solution.py:54
  19.9 0.9 fusion.35
  20.8 4.9 %all_gather.34 = bf16[16,4096]{1,0:T(8,128)(2,1)S(1)} all-gather(bf16[8,4096]{1,0:T(8,128)(2,1)S(1)} %fusion.35), channel_id=1, replica_groups=mesh['dp'=4,'section'=4,'tensor'=2] {'tensor'}, dimensions={0}, use_global_device_ids=true | all-gather | bytes 196608 | tf_op jit(solution)/shard_map/all_gather | solution.py:55
  25.7 5.2 %all-gather = bf16[1,16,4096]{2,1,0:T(8,128)(2,1)S(1)} all-gather(bf16[1,8,4096]{2,1,0:T(8,128)(2,1)} %param.12), channel_id=2, replica_groups=mesh['dp'=4,'section'=4,'tensor'=2] {'tensor'}, dimensions={1}, use_global_device_ids=true | all-gather | bytes 196608 | tf_op jit(solution)/shard_map/all_gather | solution.py:56
  30.9 7.6 %all_gather.35 = bf16[64,4096]{1,0:T(8,128)(2,1)S(1)} all-gather(bf16[16,4096]{1,0:T(8,128)(2,1)S(1)} %all_gather.34), channel_id=1, replica_groups=mesh['dp'=4,'section'=4,'tensor'=2] {'dp'}, dimensions={0}, use_global_device_ids=true | all-gather | bytes 655360 | tf_op jit(solution)/shard_map/all_gather | solution.py:62
  38.5 7.3 %all_gather.31 = bf16[64,4096]{1,0:T(8,128)(2,1)S(1)} all-gather(bf16[16,4096]{1,0:T(8,128)(2,1)S(1)} %all_gather.30), channel_id=1, replica_groups=mesh['dp'=4,'section'=4,'tensor'=2] {'dp'}, dimensions={0}, use_global_device_ids=true | all-gather | bytes 655360 | tf_op jit(solution)/shard_map/all_gather | solution.py:61
  45.8 7.6 %fusion.45 = f32[64,1376]{1,0:T(8,128)S(1)} fusion(bf16[64,4096]{1,0:T(8,128)(2,1)S(1)} %all_gather.35, bf16[4096,1376]{0,1:T(8,128)(2,1)} %param.8), kind=kOutput, calls=%fused_computation.72 | convolution fusion | flops 721420288 | bytes 12148736 | tf_op jit(solution)/shard_map/dot_general | solution.py:21
  53.5 0.0 copy-done.1
  53.5 3.5 %fusion.44 = f32[64,1376]{1,0:T(8,128)S(1)} fusion(bf16[64,4096]{1,0:T(8,128)(2,1)S(1)} %all_gather.31, bf16[4096,1376]{0,1:T(8,128)(2,1)S(1)} %copy-done.1), kind=kOutput, calls=%fused_computation.71 | convolution fusion | flops 721420288 | bytes 12148736 | tf_op jit(solution)/shard_map/dot_general | solution.py:21
  56.9 7.5 %all-gather.1 = bf16[1,64,4096]{2,1,0:T(8,128)(2,1)S(1)} all-gather(bf16[1,16,4096]{2,1,0:T(8,128)(2,1)S(1)} %all-gather), channel_id=3, replica_groups=mesh['dp'=4,'section'=4,'tensor'=2] {'dp'}, dimensions={1}, use_global_device_ids=true | all-gather | bytes 655360 | tf_op jit(solution)/shard_map/all_gather | solution.py:63
  64.4 7.7 %fusion.13 = f32[64,1376]{1,0:T(8,128)S(1)} fusion(bf16[1376,4096]{1,0:T(8,128)(2,1)} %param.10, bf16[1,64,4096]{2,1,0:T(8,128)(2,1)S(1)} %all-gather.1), kind=kOutput, calls=%fused_computation.21 | convolution fusion | flops 721420288 | bytes 12148736 | tf_op jit(solution)/shard_map/dot_general | solution.py:27
  72.1 14.0 %convolution_convert_fusion.2 = bf16[64,4096]{1,0:T(8,128)(2,1)} fusion(bf16[1376,4096]{1,0:T(8,128)(2,1)} %param.10, bf16[64,4096]{1,0:T(8,128)(2,1)S(1)} %all_gather.31, bf16[4096,1376]{0,1:T(8,128)(2,1)} %param.9, f32[64,1376]{1,0:T(8,128)S(1)} %fusion.44), kind=kOutput, calls=%fused_computation.6 | convolution fusion | flops 1443631104 | bytes 23945216 | tf_op jit(solution)/shard_map/dot_general | solution.py:72
  86.1 13.2 %fusion.10 = f32[64,4096]{1,0:T(8,128)S(1)} fusion(bf16[4096,1376]{0,1:T(8,128)(2,1)} %param.8, f32[64,1376]{1,0:T(8,128)S(1)} %fusion.13, bf16[64,4096]{1,0:T(8,128)(2,1)S(1)} %all_gather.35, bf16[4096,1376]{0,1:T(8,128)(2,1)} %param.9, f32[64,1376]{1,0:T(8,128)S(1)} %fusion.45), kind=kOutput, calls=%fused_computation.18 | convolution fusion | flops 1443721216 | bytes 24821760 | tf_op jit(solution)/shard_map/dot_general | solution.py:73
  99.3 0.0 copy-start.2
  99.4 6.6 %fusion.2 = bf16[64,4096]{1,0:T(8,128)(2,1)S(1)} fusion(f32[64,4096]{1,0:T(8,128)S(1)} %fusion.10, bf16[4096,1376]{0,1:T(8,128)(2,1)} %param.9, f32[64,1376]{1,0:T(8,128)S(1)} %fusion.13, f32[64,1376]{1,0:T(8,128)S(1)} %fusion.45), kind=kOutput, calls=%fused_computation.5 | convolution fusion | flops 722472960 | bytes 13549568 | tf_op jit(solution)/shard_map/dot_general | solution.py:76
  105.9 0.0 copy-done.2
  105.9 0.0 copy-start.3
  105.9 0.0 copy-start.4
  106.0 0.0 copy-start.5
  106.0 1.0 pad_maximum_fusion
  107.0 0.0 reduce-scatter.3.cloned.1.call-update
  107.0 0.0 reduce-scatter.5.cloned.1.call-start
  109.0 0.0 copy-done
  109.1 5.0 %all-gather.2 = bf16[1,1,16,4096]{3,2,1,0:T(8,128)(2,1)S(1)} all-gather(bf16[1,1,8,4096]{3,2,1,0:T(8,128)(2,1)S(1)} %constant_dynamic-slice_fusion), channel_id=4, replica_groups=mesh['dp'=4,'section'=4,'tensor'=2] {'tensor'}, dimensions={2}, use_global_device_ids=true | all-gather | bytes 196608 | tf_op jit(solution)/shard_map/all_gather | solution.py:58
  114.1 6.5 %all-gather.3 = bf16[1,1,64,4096]{3,2,1,0:T(8,128)(2,1)S(1)} all-gather(bf16[1,1,16,4096]{3,2,1,0:T(8,128)(2,1)S(1)} %all-gather.2), channel_id=5, replica_groups=mesh['dp'=4,'section'=4,'tensor'=2] {'dp'}, dimensions={2}, use_global_device_ids=true | all-gather | bytes 655360 | tf_op jit(solution)/shard_map/all_gather | solution.py:65
  120.6 12.0 %reduce-scatter.3.cloned.1.call-done = bf16[16,8192]{1,0:T(8,128)(2,1)} async-done(((bf16[64,8192]{1,0:T(8,128)(2,1)}), bf16[16,8192]{1,0:T(8,128)(2,1)}) %reduce-scatter.3.cloned.1.call-update) | async-done | bytes 262160 | tf_op jit(solution)/shard_map/reduce_scatter | solution.py:79
  132.6 0.0 reduce-scatter.5.cloned.1.call-update
  132.6 7.6 %fusion.11 = f32[64,1376]{1,0:T(8,128)S(1)} fusion(bf16[1376,4096]{1,0:T(8,128)(2,1)} %param.10, bf16[1,1,64,4096]{3,2,1,0:T(8,128)(2,1)S(1)} %all-gather.3), kind=kOutput, calls=%fused_computation.19 | convolution fusion | flops 721420288 | bytes 12148736 | tf_op jit(solution)/shard_map/dot_general | solution.py:27
  140.2 6.3 %reduce-scatter.5.cloned.1.call-done = bf16[8,8192]{1,0:T(8,128)(2,1)} async-done(((bf16[16,8192]{1,0:T(8,128)(2,1)}), bf16[8,8192]{1,0:T(8,128)(2,1)}) %reduce-scatter.5.cloned.1.call-update) | async-done | bytes 131088 | tf_op jit(solution)/shard_map/reduce_scatter | solution.py:85
  146.6 0.9 convert_element_type.72
  147.5 0.0 copy-done.3
  147.5 0.2 fusion.27
  147.7 0.0 copy-done.4
  147.7 0.0 copy-done.5
  147.8 0.1 fusion.28
  147.9 4.9 %all_gather.36 = bf16[16,4096]{1,0:T(8,128)(2,1)S(1)} all-gather(bf16[8,4096]{1,0:T(8,128)(2,1)S(1)} %get-tuple-element.6), channel_id=1, replica_groups=mesh['dp'=4,'section'=4,'tensor'=2] {'tensor'}, dimensions={0}, use_global_device_ids=true | all-gather | bytes 196608 | tf_op jit(solution)/shard_map/all_gather | solution.py:57
  152.8 1.3 collective-permute-start.1
  154.1 4.5 %collective-permute-start = (bf16[8,4096]{1,0:T(8,128)(2,1)S(1)}, bf16[8,4096]{1,0:T(8,128)(2,1)S(1)}, u32[]{:S(2)}, u32[]{:S(2)}) collective-permute-start(bf16[8,4096]{1,0:T(8,128)(2,1)S(1)} %get-tuple-element.8), channel_id=1, source_target_pairs={{0,2},{2,4},{4,6},{1,3},{3,5},{5,7},{8,10},{10,12},{12,14},{9,11},... | collective-permute-start | bytes 196616 | tf_op jit(solution)/shard_map/ppermute | solution.py:12
  158.7 7.1 %all_gather.37 = bf16[64,4096]{1,0:T(8,128)(2,1)S(1)} all-gather(bf16[16,4096]{1,0:T(8,128)(2,1)S(1)} %all_gather.36), channel_id=1, replica_groups=mesh['dp'=4,'section'=4,'tensor'=2] {'dp'}, dimensions={0}, use_global_device_ids=true | all-gather | bytes 655360 | tf_op jit(solution)/shard_map/all_gather | solution.py:64
  165.8 7.6 %fusion.46 = f32[64,1376]{1,0:T(8,128)S(1)} fusion(bf16[64,4096]{1,0:T(8,128)(2,1)S(1)} %all_gather.37, bf16[4096,1376]{0,1:T(8,128)(2,1)} %param.8), kind=kOutput, calls=%fused_computation.73 | convolution fusion | flops 721420288 | bytes 12148736 | tf_op jit(solution)/shard_map/dot_general | solution.py:21
  173.5 17.8 %fusion = bf16[1,4096,1376]{1,2,0:T(8,128)(2,1)} fusion(bf16[64,4096]{1,0:T(8,128)(2,1)S(1)} %all_gather.37, f32[64,1376]{1,0:T(8,128)S(1)} %fusion.11, bf16[4096,1376]{0,1:T(8,128)(2,1)} %param.9, f32[64,1376]{1,0:T(8,128)S(1)} %fusion.46), kind=kOutput, calls=%fused_computation.2 | convolution fusion | flops 1449357312 | bytes 23773184 | tf_op jit(solution)/shard_map/dot_general | solution.py:39
  191.2 6.0 %fusion.1 = bf16[1,4096,1376]{1,2,0:T(8,128)(2,1)} fusion(bf16[64,4096]{1,0:T(8,128)(2,1)S(1)} %all_gather.37, f32[64,1376]{1,0:T(8,128)S(1)} %fusion.11, f32[64,1376]{1,0:T(8,128)S(1)} %fusion.46), kind=kOutput, calls=%fused_computation.3 | convolution fusion | flops 727584768 | bytes 12500992 | tf_op jit(solution)/shard_map/dot_general | solution.py:39
  197.2 0.0 collective-permute-done.1
  197.2 0.0 collective-permute-done
  197.3 0.6 copy.14
  197.9 0.6 copy.15
  (4 shorter events, 0.0 us)
Async XLA Ops:
  7.2 101.9 %copy-start = (bf16[1,4,8,4096]{3,2,1,0:T(8,128)(2,1)S(1)}, bf16[1,4,8,4096]{3,2,1,0:T(8,128)(2,1)}, u32[]{:S(2)}) copy-start(bf16[1,4,8,4096]{3,2,1,0:T(8,128)(2,1)} %param.14) | copy-start | bytes 786436
  7.2 125.4 %reduce-scatter.3.cloned.1.call-start = ((), (), s32[]{:S(2)}) async-start(), calls=%async_computation.2 | async-start | bytes 1310720 | tf_op jit(solution)/shard_map/reduce_scatter | solution.py:79
  11.5 41.9 %copy-start.1 = (bf16[4096,1376]{0,1:T(8,128)(2,1)S(1)}, bf16[4096,1376]{0,1:T(8,128)(2,1)}, u32[]{:S(2)}) copy-start(bf16[4096,1376]{0,1:T(8,128)(2,1)} %param.8) | copy-start | bytes 33816580
  99.3 6.6 %copy-start.2 = (bf16[64,4096]{1,0:T(8,128)(2,1)S(1)}, bf16[64,4096]{1,0:T(8,128)(2,1)}, u32[]{:S(2)}) copy-start(bf16[64,4096]{1,0:T(8,128)(2,1)} %convolution_convert_fusion.2) | copy-start | bytes 1572868
  105.9 41.6 %copy-start.3 = (bf16[1,4,8,4096]{3,2,1,0:T(8,128)(2,1)S(1)}, bf16[1,4,8,4096]{3,2,1,0:T(8,128)(2,1)}, u32[]{:S(2)}) copy-start(bf16[1,4,8,4096]{3,2,1,0:T(8,128)(2,1)} %param.13) | copy-start | bytes 786436
  105.9 41.8 %copy-start.4 = (bf16[1,8,4096]{2,1,0:T(8,128)(2,1)S(1)}, bf16[1,8,4096]{2,1,0:T(8,128)(2,1)}, u32[]{:S(2)}) copy-start(bf16[1,8,4096]{2,1,0:T(8,128)(2,1)} %param.11) | copy-start | bytes 196612
  106.0 41.8 %copy-start.5 = (bf16[1,8,4096]{2,1,0:T(8,128)(2,1)S(1)}, bf16[1,8,4096]{2,1,0:T(8,128)(2,1)}, u32[]{:S(2)}) copy-start(bf16[1,8,4096]{2,1,0:T(8,128)(2,1)} %param.12) | copy-start | bytes 196612
  107.0 39.6 %reduce-scatter.5.cloned.1.call-start = ((), (), s32[]{:S(2)}) async-start(), calls=%async_computation.3 | async-start | bytes 393216 | tf_op jit(solution)/shard_map/reduce_scatter | solution.py:85
  152.8 44.4 %collective-permute-start.1 = (bf16[8,4096]{1,0:T(8,128)(2,1)S(1)}, bf16[8,4096]{1,0:T(8,128)(2,1)S(1)}, u32[]{:S(2)}, u32[]{:S(2)}) collective-permute-start(bf16[8,4096]{1,0:T(8,128)(2,1)S(1)} %get-tuple-element.7), channel_id=1, source_target_pairs={{2,0},{4,2},{6,4},{3,1},{5,3},{7,5},{10,8},{12,10},{14,12},{11,9},... | collective-permute-start | bytes 196616 | tf_op jit(solution)/shard_map/ppermute | solution.py:12
  154.1 43.1 %collective-permute-start = (bf16[8,4096]{1,0:T(8,128)(2,1)S(1)}, bf16[8,4096]{1,0:T(8,128)(2,1)S(1)}, u32[]{:S(2)}, u32[]{:S(2)}) collective-permute-start(bf16[8,4096]{1,0:T(8,128)(2,1)S(1)} %get-tuple-element.8), channel_id=1, source_target_pairs={{0,2},{2,4},{4,6},{1,3},{3,5},{5,7},{8,10},{10,12},{12,14},{9,11},... | collective-permute-start | bytes 196616 | tf_op jit(solution)/shard_map/ppermute | solution.py:12
Sparse Core Ops, SparseCore 0:
  107.2 25.3 reduce-scatter.2
  134.8 11.7 reduce-scatter.4
where the time goes:
time: 206 us; the launch traced here: 205 us
  matrix products  91.7 us (45%)
  blocking collectives  62.1 us (30%)
  waiting for transfers between devices  18.4 us (9%)
  between operations  18.1 us (9%)
  other arithmetic  6.55 us (3%)
  starting transfers between devices  5.91 us (3%)
  local copies, waits for them, and re-layouts  2.63 us (1%)
    dot_general x2, matrix products, contract_rows(): lax.dot_general(left, right, (((0,), (0,)), ((), ())), preferred_element_...  23.8 us
    dot_general x3, matrix products, gated(): gate_pre = jnp.dot(normed, w_gate, preferred_element_type=jnp.float32)  18.7 us
    dot_general x2, matrix products, back_gates(): lax.dot_general(cotangent, w_down, (((1,), (1,)), ((), ())), preferred_el...  15.3 us
    dot_general x1, matrix products, body(): branch = jnp.dot(act_front, weight_down, preferred_element_type=jnp.float32)  14 us
    dot_general x1, matrix products, body(): lax.dot_general(dgate_back, weight_gate, (((1,), (1,)), ((), ())), prefer...  13.2 us
    reduce_scatter x1, waiting for transfers between devices, body(): lax.psum_scatter(jnp.concatenate([branch, d_norm], axis=1).astype(jnp.bfl...  12 us
    all_gather x1, blocking collectives, body(): lax.all_gather(in_group[1], 'dp', axis=0, tiled=True)  7.61 us
    all_gather x1, blocking collectives, body(): lax.all_gather(in_group[2], 'dp', axis=0, tiled=True)  7.46 us
  transfers between devices with their start and end apart: 4, of which 2 were waited for; matrix products, arithmetic and copies ran while one was open for 19% of the time, Pallas kernels for 0%

commit v1 on v0

--- a/solution.py
+++ b/solution.py
@@ -1,6 +1,8 @@
 import jax
 import jax.numpy as jnp
 from jax import lax
+from jax.experimental import pallas as pl
+from jax.experimental.pallas import tpu as pltpu
 from jax.sharding import PartitionSpec as P
 
 EPS = 0.5
@@ -41,7 +43,7 @@
     )
 
 
-def body(weight_gate, weight_up, weight_down, acts_in, grads_in, saved_acts, saved_grads, plan):
+def plain_body(weight_gate, weight_up, weight_down, acts_in, grads_in, saved_acts, saved_grads, plan):
     front_rows = acts_in[0]
     cot_back = grads_in[0]
     back_rows = lax.dynamic_index_in_dim(saved_acts[0], plan[0, 0], 0, keepdims=False)
@@ -101,6 +103,388 @@
     return (next_acts[None], next_grads[None], grad_gate[None], grad_up[None])
 
 
+STEP = 512
+NT = (((1,), (1,)), ((), ()))
+F32 = jnp.float32
+BF16 = jnp.bfloat16
+FRONT, BACK, COT_BACK, COT_LATE, LATE = range(5)
+
+
+def tick_kernel(
+    plan, w_gate, w_up, w_down, acts_in, grads_in, saved_acts, saved_grads,
+    next_acts, next_grads, late_out, dgate_out, dup_out,
+    gate_v, up_v, down_v, blocks, x_fb, x_gh, acc_gate, acc_up, acc_act, act_f, dgate_b, dup_b,
+    part, recv_core, held, recv_first, held_next, recv_second, out_rows, in_rows,
+    sem_gate, sem_up, sem_down, g_send, g_recv, r_send, r_recv, s_send, s_recv,
+):
+    dp, y, section = lax.axis_index("dp"), lax.axis_index("tensor"), lax.axis_index("section")
+    sections = lax.axis_size("section")
+    x, c = dp // 2, dp % 2
+    rows, width = acts_in.shape
+    steps = width // STEP
+    down_cols = width // sem_down.shape[0]
+    first_dp = ((1 - x) * (1 - c) + x * c) * 2 + c
+    first_y = y * (1 - c) + (1 - y) * c
+    second_dp = (x * (1 - c) + (1 - x) * c) * 2 + c
+    second_y = (1 - y) * (1 - c) + y * c
+    first = {"dp": first_dp, "tensor": first_y}
+    second = {"dp": second_dp, "tensor": second_y}
+    partner = {"dp": x * 2 + 1 - c}
+    after = {"section": (section + 1) % sections}
+    before = {"section": (section + sections - 1) % sections}
+    own_b = dp * 2 + y
+    first_b = first_dp * 2 + first_y
+    second_b = second_dp * 2 + second_y
+    far_b = ((1 - x) * 2 + c) * 2 + 1 - y
+    other = 2 - 4 * c
+
+    def gate_copy(k):
+        at = pl.ds(pl.multiple_of(k * STEP, STEP), STEP)
+        return pltpu.make_async_copy(w_gate.at[at], gate_v.at[at], sem_gate.at[k])
+
+    def up_copy(k):
+        at = pl.ds(pl.multiple_of(k * STEP, STEP), STEP)
+        return pltpu.make_async_copy(w_up.at[at], up_v.at[at], sem_up.at[k])
+
+    def down_copy(k):
+        at = pl.ds(k * down_cols, down_cols)
+        return pltpu.make_async_copy(w_down.at[:, at], down_v.at[:, at], sem_down.at[k])
+
+    def start_weights(k, carry):
+        gate_copy(k).start()
+        up_copy(k).start()
+        return carry
+
+    lax.fori_loop(0, steps, start_weights, 0)
+    for k in range(sem_down.shape[0]):
+        down_copy(k).start()
+
+    barrier = pltpu.get_barrier_semaphore()
+    for peer in (first, second, partner, after, before):
+        pl.semaphore_signal(barrier, inc=1, device_id=peer, device_id_type=pl.DeviceIdType.MESH)
+
+    back_slot, late_slot = plan[0, 0], plan[0, 1]
+    blocks[FRONT, own_b] = rms_scale(acts_in[...].astype(F32)).astype(BF16)
+    blocks[BACK, own_b] = rms_scale(saved_acts[back_slot].astype(F32)).astype(BF16)
+    blocks[COT_BACK, own_b] = grads_in[...]
+    blocks[COT_LATE, own_b] = saved_grads[late_slot]
+    blocks[LATE, own_b] = rms_scale(saved_acts[late_slot].astype(F32)).astype(BF16)
+    pl.semaphore_wait(barrier, 5)
+
+    def remote(src, dst, send, recv, peer):
+        return pltpu.make_async_remote_copy(
+            src_ref=src, dst_ref=dst, send_sem=send, recv_sem=recv,
+            device_id=peer, device_id_type=pl.DeviceIdType.MESH,
+        )
+
+    def block_copy(a, b, slot, peer):
+        return remote(blocks.at[a, b], blocks.at[a, b], g_send.at[a, slot], g_recv.at[a, slot], peer)
+
+    def arrived(a, b, slot):
+        block_copy(a, b, slot, partner).wait_recv()
+
+    def send_own(a):
+        block_copy(a, own_b, 0, first).start()
+        block_copy(a, own_b, 1, second).start()
+        block_copy(a, own_b, 3, partner).start()
+
+    def relay(a):
+        arrived(a, first_b, 0)
+        block_copy(a, first_b, 2, second).start()
+        block_copy(a, first_b, 4, partner).start()
+
+    def finish(a):
+        arrived(a, second_b, 1)
+        block_copy(a, second_b, 5, partner).start()
+        arrived(a, far_b, 2)
+        block_copy(a, far_b, 6, partner).start()
+        for slot, b in ((3, own_b), (4, second_b), (5, first_b), (6, far_b)):
+            arrived(a, b + other, slot)
+
+    def assemble(a, out, offset):
+        def move(k, carry):
+            at = pl.ds(pl.multiple_of(k * STEP, STEP), STEP)
+            piece = blocks[a, :, :, at].astype(F32)
+            out[offset : offset + piece.shape[0] * rows, at] = piece.reshape(-1, STEP).astype(BF16)
+            return carry
+
+        lax.fori_loop(0, steps, move, 0)
+
+    tokens = blocks.shape[1] * rows
+    send_own(FRONT)
+    send_own(BACK)
+    relay(FRONT)
+    send_own(COT_BACK)
+    relay(BACK)
+    send_own(COT_LATE)
+    finish(FRONT)
+    assemble(FRONT, x_fb, 0)
+    finish(BACK)
+    assemble(BACK, x_fb, tokens)
+
+    def up_front(k, carry):
+        gate_copy(k).wait()
+        up_copy(k).wait()
+        at = pl.ds(pl.multiple_of(k * STEP, STEP), STEP)
+        piece = x_fb[:, at]
+        acc_gate[...] += jnp.dot(piece, gate_v[at, :], preferred_element_type=F32)
+        acc_up[...] += jnp.dot(piece, up_v[at, :], preferred_element_type=F32)
+        return carry
+
+    acc_gate[...] = jnp.zeros_like(acc_gate)
+    acc_up[...] = jnp.zeros_like(acc_up)
+    lax.fori_loop(0, steps // 2, up_front, 0)
+    relay(COT_BACK)
+    send_own(LATE)
+    relay(COT_LATE)
+    lax.fori_loop(steps // 2, steps, up_front, 0)
+    finish(COT_BACK)
+    assemble(COT_BACK, x_gh, 0)
+    relay(LATE)
+    finish(COT_LATE)
+    assemble(COT_LATE, x_gh, tokens)
+
+    for k in range(sem_down.shape[0]):
+        down_copy(k).wait()
+
+    def d_act_step(k, carry):
+        at = pl.ds(pl.multiple_of(k * STEP, STEP), STEP)
+        acc_act[...] += lax.dot_general(x_gh[:, at], down_v[:, at], NT, preferred_element_type=F32)
+        return carry
+
+    acc_act[...] = jnp.zeros_like(acc_act)
+    lax.fori_loop(0, steps, d_act_step, 0)
+
+    def back_of(d_act, gate_pre, up_pre):
+        sigmoid_gate = jax.nn.sigmoid(gate_pre)
+        d_up = (d_act * gate_pre * sigmoid_gate).astype(BF16)
+        d_gate = (d_act * up_pre * sigmoid_gate * (1.0 + gate_pre * (1.0 - sigmoid_gate))).astype(BF16)
+        return d_gate, d_up
+
+    group = 16
+
+    def pointwise(i, carry):
+        at = pl.ds(pl.multiple_of(i * group, group), group)
+        low = pl.ds(pl.multiple_of(tokens + i * group, group), group)
+        dgate_b[at, :], dup_b[at, :] = back_of(acc_act[at, :], acc_gate[low, :], acc_up[low, :])
+        gate_pre = acc_gate[at, :]
+        act_f[at, :] = (gate_pre * jax.nn.sigmoid(gate_pre) * acc_up[at, :]).astype(BF16)
+        return carry
+
+    lax.fori_loop(0, tokens // group, pointwise, 0)
+
+    def put_part(r, at, total):
+        for b in range(8):
+            part[r, (b // 2) % 2, b // 4, b % 2, :, at] = total[b * rows : (b + 1) * rows].astype(BF16)
+
+    def d_norm_step(k, carry):
+        at = pl.ds(pl.multiple_of(k * STEP, STEP), STEP)
+        total = lax.dot_general(dgate_b[...], gate_v[at, :], NT, preferred_element_type=F32)
+        total += lax.dot_general(dup_b[...], up_v[at, :], NT, preferred_element_type=F32)
+        put_part(0, at, total)
+        return carry
+
+    def branch_step(k, carry):
+        at = pl.ds(pl.multiple_of(k * STEP, STEP), STEP)
+        put_part(1, at, jnp.dot(act_f[...], down_v[:, at], preferred_element_type=F32))
+        return carry
+
+    mine_first = x * (1 - c) + y * c
+    mine_second = y * (1 - c) + x * c
+
+    def core_copy(r):
+        return remote(part.at[r, 1 - c], recv_core.at[r], r_send.at[r, 0], r_recv.at[r, 0], partner)
+
+    def first_copy(r):
+        return remote(held.at[r, 1 - mine_first], recv_first.at[r], r_send.at[r, 1], r_recv.at[r, 1], first)
+
+    def second_copy(r):
+        return remote(held_next.at[r, 1 - mine_second], recv_second.at[r], r_send.at[r, 2], r_recv.at[r, 2], second)
+
+    def add_core(r):
+        core_copy(r).wait_recv()
+        for f in range(2):
+            for s in range(2):
+                at_x = f * (1 - c) + s * c
+                at_y = s * (1 - c) + f * c
+                mine = part[r, c, at_x, at_y].astype(F32)
+                held[r, f, s] = (mine + recv_core[r, at_x, at_y].astype(F32)).astype(BF16)
+        first_copy(r).start()
+
+    def add_first(r):
+        first_copy(r).wait_recv()
+        for s in range(2):
+            mine = held[r, mine_first, s].astype(F32)
+            held_next[r, s] = (mine + recv_first[r, s].astype(F32)).astype(BF16)
+        second_copy(r).start()
+
+    def add_second(r):
+        second_copy(r).wait_recv()
+        return held_next[r, mine_second].astype(F32) + recv_second[r].astype(F32)
+
+    def shift(r):
+        return remote(out_rows.at[r], in_rows.at[r], s_send.at[r], s_recv.at[r], before if r == 0 else after)
+
+    lax.fori_loop(0, steps, d_norm_step, 0)
+    core_copy(0).start()
+    lax.fori_loop(0, steps, branch_step, 0)
+    core_copy(1).start()
+    add_core(0)
+    finish(LATE)
+    assemble(LATE, late_out, 0)
+
+    def up_late(k, carry):
+        at = pl.ds(pl.multiple_of(k * STEP, STEP), STEP)
+        piece = late_out[:, at]
+        acc_gate[:tokens] += jnp.dot(piece, gate_v[at, :], preferred_element_type=F32)
+        acc_up[:tokens] += jnp.dot(piece, up_v[at, :], preferred_element_type=F32)
+        return carry
+
+    acc_gate[:tokens] = jnp.zeros((tokens, acc_gate.shape[1]), F32)
+    acc_up[:tokens] = jnp.zeros((tokens, acc_up.shape[1]), F32)
+    add_core(1)
+    lax.fori_loop(0, steps // 2, up_late, 0)
+    add_first(0)
+    add_first(1)
+    lax.fori_loop(steps // 2, steps, up_late, 0)
+
+    d_norm = add_second(0)
+    rows_b = saved_acts[back_slot].astype(F32)
+    scale = lax.rsqrt(jnp.mean(rows_b * rows_b, axis=-1, keepdims=True) + EPS)
+    along = jnp.mean(d_norm * rows_b, axis=-1, keepdims=True)
+    d_input = d_norm * scale - rows_b * (scale * scale * scale * along)
+    out_rows[0] = (grads_in[...].astype(F32) + d_input).astype(BF16)
+
+    @pl.when(section > 0)
+    def _():
+        shift(0).start()
+
+    out_rows[1] = (acts_in[...].astype(F32) + add_second(1)).astype(BF16)
+
+    @pl.when(section < sections - 1)
+    def _():
+        shift(1).start()
+
+    def pointwise_late(i, carry):
+        at = pl.ds(pl.multiple_of(i * group, group), group)
+        low = pl.ds(pl.multiple_of(tokens + i * group, group), group)
+        dgate_out[at, :], dup_out[at, :] = back_of(acc_act[low, :], acc_gate[at, :], acc_up[at, :])
+        return carry
+
+    lax.fori_loop(0, tokens // group, pointwise_late, 0)
+
+    @pl.when(section < sections - 1)
+    def _():
+        shift(0).wait_recv()
+        next_grads[...] = in_rows[0]
+
+    @pl.when(section == sections - 1)
+    def _():
+        next_grads[...] = jnp.zeros_like(next_grads)
+
+    @pl.when(section > 0)
+    def _():
+        shift(1).wait_recv()
+        next_acts[...] = in_rows[1]
+        shift(0).wait_send()
+
+    @pl.when(section == 0)
+    def _():
+        next_acts[...] = jnp.zeros_like(next_acts)
+
+    @pl.when(section < sections - 1)
+    def _():
+        shift(1).wait_send()
+
+    for r in range(2):
+        core_copy(r).wait_send()
+        first_copy(r).wait_send()
+        second_copy(r).wait_send()
+    for a in range(5):
+        for slot in range(7):
+            block_copy(a, own_b, slot, partner).wait_send()
+
+
+def outer_kernel(late, d_gate, d_up, grad_gate, grad_up):
+    left = late[...]
+    grad_gate[...] = contract_rows(left, d_gate[...]).astype(BF16)
+    grad_up[...] = contract_rows(left, d_up[...]).astype(BF16)
+
+
+def outer(late, d_gate, d_up):
+    tokens, width = late.shape
+    hidden = d_gate.shape[1]
+    whole = pl.BlockSpec((tokens, hidden), lambda i: (0, 0))
+    tile = pl.BlockSpec((STEP, hidden), lambda i: (i, 0))
+    return pl.pallas_call(
+        outer_kernel,
+        grid=(width // STEP,),
+        out_shape=(jax.ShapeDtypeStruct((width, hidden), BF16),) * 2,
+        in_specs=[pl.BlockSpec((tokens, STEP), lambda i: (0, i)), whole, whole],
+        out_specs=(tile, tile),
+        cost_estimate=pl.CostEstimate(
+            flops=4 * tokens * width * hidden, bytes_accessed=4 * width * hidden, transcendentals=0
+        ),
+    )(late, d_gate, d_up)
+
+
+def body(weight_gate, weight_up, weight_down, acts_in, grads_in, saved_acts, saved_grads, plan):
+    width, hidden = weight_gate.shape
+    rows = acts_in.shape[1]
+    blocks = 8
+    tokens = rows * blocks
+    vmem = pl.BlockSpec(memory_space=pltpu.VMEM)
+    hbm = pl.BlockSpec(memory_space=pl.ANY)
+    dma = pltpu.SemaphoreType.DMA
+    small = jax.ShapeDtypeStruct((rows, width), BF16)
+    narrow = jax.ShapeDtypeStruct((tokens, hidden), BF16)
+    next_acts, next_grads, late, d_gate, d_up = pl.pallas_call(
+        tick_kernel,
+        out_shape=(small, small, jax.ShapeDtypeStruct((tokens, width), BF16), narrow, narrow),
+        in_specs=[pl.BlockSpec(memory_space=pltpu.SMEM), hbm, hbm, hbm, vmem, vmem, vmem, vmem],
+        out_specs=(vmem,) * 5,
+        scratch_shapes=[
+            pltpu.VMEM((width, hidden), BF16),
+            pltpu.VMEM((width, hidden), BF16),
+            pltpu.VMEM((hidden, width), BF16),
+            pltpu.VMEM((5, blocks, rows, width), BF16),
+            pltpu.VMEM((2 * tokens, width), BF16),
+            pltpu.VMEM((2 * tokens, width), BF16),
+            pltpu.VMEM((2 * tokens, hidden), F32),
+            pltpu.VMEM((2 * tokens, hidden), F32),
+            pltpu.VMEM((2 * tokens, hidden), F32),
+            pltpu.VMEM((tokens, hidden), BF16),
+            pltpu.VMEM((tokens, hidden), BF16),
+            pltpu.VMEM((tokens, hidden), BF16),
+            pltpu.VMEM((2, 2, 2, 2, rows, width), BF16),
+            pltpu.VMEM((2, 2, 2, rows, width), BF16),
+            pltpu.VMEM((2, 2, 2, rows, width), BF16),
+            pltpu.VMEM((2, 2, rows, width), BF16),
+            pltpu.VMEM((2, 2, rows, width), BF16),
+            pltpu.VMEM((2, rows, width), BF16),
+            pltpu.VMEM((2, rows, width), BF16),
+            pltpu.VMEM((2, rows, width), BF16),
+            dma((width // STEP,)),
+            dma((width // STEP,)),
+            dma((4,)),
+            dma((5, 7)),
+            dma((5, 7)),
+            dma((2, 3)),
+            dma((2, 3)),
+            dma((2,)),
+            dma((2,)),
+        ],
+        compiler_params=pltpu.CompilerParams(
+            collective_id=0, has_side_effects=True, vmem_limit_bytes=64 * 1024 * 1000
+        ),
+    )(
+        plan, weight_gate, weight_up, weight_down,
+        acts_in[0], grads_in[0], saved_acts[0], saved_grads[0],
+    )
+    grad_gate, grad_up = outer(late, d_gate, d_up)
+    return (next_acts[None], next_grads[None], grad_gate[None], grad_up[None])
+
+
 def solution(mesh):
     placed = (
         P(None, ("dp", "tensor")),
@@ -112,8 +496,16 @@
         P("section", None, ("dp", "tensor"), None),
         P("section", None),
     )
+
+    def chosen(*arrays):
+        width = arrays[0].shape[0]
+        rows = arrays[3].shape[1]
+        square = mesh.shape["dp"] == 4 and mesh.shape["tensor"] == 2
+        fits = square and rows % 8 == 0 and width % (2 * STEP) == 0 and arrays[0].shape[1] % 16 == 0
+        return (body if fits else plain_body)(*arrays)
+
     return jax.shard_map(
-        body,
+        chosen,
         mesh=mesh,
         in_specs=placed,
         out_specs=(

time: 206 us -> 129 us (0.63)
  matrix products: 91.7 us -> 0 us
  Pallas kernels: 0 us -> 64.7 us
  blocking collectives: 62.1 us -> 0 us
  local copies, waits for them, and re-layouts: 2.63 us -> 61.6 us
  waiting for transfers between devices: 18.4 us -> 0 us
  between operations: 18.1 us -> 0.64 us
  other arithmetic: 6.55 us -> 0 us
  starting transfers between devices: 5.91 us -> 0 us
    dot_general x10 -> x0, matrix products: 91.7 us -> none  [the longest x2 23.8 us: contract_rows(): lax.dot_general(left, right, (((0,), (0,)), ((), ())), preferred_element_...]
    pallas_call x0 -> x2, Pallas kernels: none -> 64.7 us  [the longest x1 53.8 us: body(): pl.pallas_call(tick_kernel, out_shape=(small, small, jax.ShapeDtypeStruct...]
    all_gather x10 -> x0, blocking collectives: 62.1 us -> none  [the longest x1 7.61 us: body(): lax.all_gather(in_group[1], 'dp', axis=0, tiled=True)]
    unnamed x14 -> x10, local copies, waits for them, and re-layouts: 1.3 us -> 61.6 us
    reduce_scatter x2 -> x0, waiting for transfers between devices: 18.4 us -> none  [the longest x1 12 us: body(): lax.psum_scatter(jnp.concatenate([branch, d_norm], axis=1).astype(jnp.bfl...]
    ppermute x2 -> x0, starting transfers between devices: 5.83 us -> none  [shifted(): return lax.ppermute(block, axis, route)]
    convert_element_type x4 -> x0, other arithmetic: 3.14 us -> none  [the longest x1 1.18 us: body(): norm_front = rms_scale(front_rows.astype(jnp.float32)).astype(jnp.bfloat16)]
    reduce_sum x3 -> x0, other arithmetic: 2.34 us -> none  [rms_scale(): mean_sq = jnp.mean(row_block * row_block, axis=-1, keepdims=True)]
  transfers between devices with their start and end apart: 4 -> 0, of which waited for: 2 -> 0; matrix products, arithmetic and copies ran while one was open for 19% -> 0% of each run, Pallas kernels for 0% -> 0%
where the time goes in v1:
time: 129 us; the launch traced here: 127 us
  Pallas kernels  64.7 us (50%)
  local copies, waits for them, and re-layouts  61.6 us (48%)
    unnamed x10, local copies, waits for them, and re-layouts  61.6 us
    pallas_call x1, Pallas kernels, body(): pl.pallas_call(tick_kernel, out_shape=(small, small, jax.ShapeDtypeStruct...  53.8 us
    pallas_call x1, Pallas kernels, outer(): pl.pallas_call(outer_kernel, grid=(width // STEP,), out_shape=(jax.ShapeD...  10.9 us

profile of v1, /device:TPU:0, one launch (start us, length us, event | category | flops | bytes accessed | tf_op | source)
XLA Modules:
  0.0 126.9 jit_solution(3544428075699648284)
XLA Ops:
  0.6 15.3 %copy.12.w_gate = bf16[4096,1376]{1,0:T(8,128)(2,1)} copy(bf16[4096,1376]{0,1:T(8,128)(2,1)} %param.8) | data formatting | bytes 22544384 | tf_op args[0]
  15.9 15.1 %copy.13.w_up = bf16[4096,1376]{1,0:T(8,128)(2,1)} copy(bf16[4096,1376]{0,1:T(8,128)(2,1)} %param.9) | data formatting | bytes 22544384 | tf_op args[1]
  31.0 53.8 %shard_map.111 = (bf16[8,4096]{1,0:T(8,128)(2,1)}, bf16[8,4096]{1,0:T(8,128)(2,1)}, bf16[64,4096]{1,0:T(8,128)(2,1)}, bf16[64,1376]{1,0:T(8,128)(2,1)}, bf16[64,1376]{1,0:T(8,128)(2,1)}) custom-call(s32[1,2]{1,0:T(1,128)} %plan.1, bf16[4096,1376]{1,0:T(8,128)(2,1)} %copy.12.w_gate, bf16[4096,1376]{1,0:T(8,128)(2,1)} %copy.13.w_up, ...), custom_call_target="tpu_custom_call" | custom-call | tf_op jit(solution)/shard_map/pallas_call | solution.py:441
  84.9 10.9 %shard_map.112 = (bf16[4096,1376]{1,0:T(8,128)(2,1)}, bf16[4096,1376]{1,0:T(8,128)(2,1)}) custom-call(bf16[64,4096]{1,0:T(8,128)(2,1)} %get-tuple-element.13.late, bf16[64,1376]{1,0:T(8,128)(2,1)} %get-tuple-element.14.d_gate, bf16[64,1376]{1,0:T(8,128)(2,1)} %get-tuple-element.15.d_up), custom_call_target="tpu_custom_call" | custom-call | flops 1442840576 | bytes 22544384 | tf_op jit(solution)/shard_map/pallas_call | solution.py:419
  95.8 14.9 %copy.14 = bf16[1,4096,1376]{1,2,0:T(8,128)(2,1)} copy(bf16[1,4096,1376]{2,1,0:T(8,128)(2,1)} %bitcast.9) | data formatting | bytes 22544384
  110.7 0.0 copy-start.1
  110.7 0.0 copy-start
  110.7 15.0 %copy.15 = bf16[1,4096,1376]{1,2,0:T(8,128)(2,1)} copy(bf16[1,4096,1376]{2,1,0:T(8,128)(2,1)} %bitcast.8) | data formatting | bytes 22544384
  125.7 0.0 copy-done.1
  125.7 0.6 copy.18
  126.3 0.0 copy-done
  126.3 0.6 copy.19
Async XLA Ops:
  110.7 15.0 %copy-start.1 = (bf16[8,4096]{1,0:T(8,128)(2,1)S(1)}, bf16[8,4096]{1,0:T(8,128)(2,1)}, u32[]{:S(2)}) copy-start(bf16[8,4096]{1,0:T(8,128)(2,1)} %get-tuple-element.11) | copy-start | bytes 196612
  110.7 15.6 %copy-start = (bf16[8,4096]{1,0:T(8,128)(2,1)S(1)}, bf16[8,4096]{1,0:T(8,128)(2,1)}, u32[]{:S(2)}) copy-start(bf16[8,4096]{1,0:T(8,128)(2,1)} %get-tuple-element.12) | copy-start | bytes 196612

commit v2 on v1

--- a/solution.py
+++ b/solution.py
@@ -140,11 +140,11 @@
 
     def gate_copy(k):
         at = pl.ds(pl.multiple_of(k * STEP, STEP), STEP)
-        return pltpu.make_async_copy(w_gate.at[at], gate_v.at[at], sem_gate.at[k])
+        return pltpu.make_async_copy(w_gate.at[:, at], gate_v.at[:, at], sem_gate.at[k])
 
     def up_copy(k):
         at = pl.ds(pl.multiple_of(k * STEP, STEP), STEP)
-        return pltpu.make_async_copy(w_up.at[at], up_v.at[at], sem_up.at[k])
+        return pltpu.make_async_copy(w_up.at[:, at], up_v.at[:, at], sem_up.at[k])
 
     def down_copy(k):
         at = pl.ds(k * down_cols, down_cols)
@@ -227,8 +227,8 @@
         up_copy(k).wait()
         at = pl.ds(pl.multiple_of(k * STEP, STEP), STEP)
         piece = x_fb[:, at]
-        acc_gate[...] += jnp.dot(piece, gate_v[at, :], preferred_element_type=F32)
-        acc_up[...] += jnp.dot(piece, up_v[at, :], preferred_element_type=F32)
+        acc_gate[...] += lax.dot_general(piece, gate_v[:, at], NT, preferred_element_type=F32)
+        acc_up[...] += lax.dot_general(piece, up_v[:, at], NT, preferred_element_type=F32)
         return carry
 
     acc_gate[...] = jnp.zeros_like(acc_gate)
@@ -279,8 +279,8 @@
 
     def d_norm_step(k, carry):
         at = pl.ds(pl.multiple_of(k * STEP, STEP), STEP)
-        total = lax.dot_general(dgate_b[...], gate_v[at, :], NT, preferred_element_type=F32)
-        total += lax.dot_general(dup_b[...], up_v[at, :], NT, preferred_element_type=F32)
+        total = jnp.dot(dgate_b[...], gate_v[:, at], preferred_element_type=F32)
+        total += jnp.dot(dup_b[...], up_v[:, at], preferred_element_type=F32)
         put_part(0, at, total)
         return carry
 
@@ -336,8 +336,8 @@
     def up_late(k, carry):
         at = pl.ds(pl.multiple_of(k * STEP, STEP), STEP)
         piece = late_out[:, at]
-        acc_gate[:tokens] += jnp.dot(piece, gate_v[at, :], preferred_element_type=F32)
-        acc_up[:tokens] += jnp.dot(piece, up_v[at, :], preferred_element_type=F32)
+        acc_gate[:tokens] += lax.dot_general(piece, gate_v[:, at], NT, preferred_element_type=F32)
+        acc_up[:tokens] += lax.dot_general(piece, up_v[:, at], NT, preferred_element_type=F32)
         return carry
 
     acc_gate[:tokens] = jnp.zeros((tokens, acc_gate.shape[1]), F32)
@@ -406,20 +406,20 @@
 
 
 def outer_kernel(late, d_gate, d_up, grad_gate, grad_up):
-    left = late[...]
-    grad_gate[...] = contract_rows(left, d_gate[...]).astype(BF16)
-    grad_up[...] = contract_rows(left, d_up[...]).astype(BF16)
+    right = late[...]
+    grad_gate[...] = contract_rows(d_gate[...], right).astype(BF16)
+    grad_up[...] = contract_rows(d_up[...], right).astype(BF16)
 
 
 def outer(late, d_gate, d_up):
     tokens, width = late.shape
     hidden = d_gate.shape[1]
     whole = pl.BlockSpec((tokens, hidden), lambda i: (0, 0))
-    tile = pl.BlockSpec((STEP, hidden), lambda i: (i, 0))
+    tile = pl.BlockSpec((hidden, STEP), lambda i: (0, i))
     return pl.pallas_call(
         outer_kernel,
         grid=(width // STEP,),
-        out_shape=(jax.ShapeDtypeStruct((width, hidden), BF16),) * 2,
+        out_shape=(jax.ShapeDtypeStruct((hidden, width), BF16),) * 2,
         in_specs=[pl.BlockSpec((tokens, STEP), lambda i: (0, i)), whole, whole],
         out_specs=(tile, tile),
         cost_estimate=pl.CostEstimate(
@@ -444,8 +444,8 @@
         in_specs=[pl.BlockSpec(memory_space=pltpu.SMEM), hbm, hbm, hbm, vmem, vmem, vmem, vmem],
         out_specs=(vmem,) * 5,
         scratch_shapes=[
-            pltpu.VMEM((width, hidden), BF16),
-            pltpu.VMEM((width, hidden), BF16),
+            pltpu.VMEM((hidden, width), BF16),
+            pltpu.VMEM((hidden, width), BF16),
             pltpu.VMEM((hidden, width), BF16),
             pltpu.VMEM((5, blocks, rows, width), BF16),
             pltpu.VMEM((2 * tokens, width), BF16),
@@ -478,11 +478,11 @@
             collective_id=0, has_side_effects=True, vmem_limit_bytes=64 * 1024 * 1000
         ),
     )(
-        plan, weight_gate, weight_up, weight_down,
+        plan, weight_gate.T, weight_up.T, weight_down,
         acts_in[0], grads_in[0], saved_acts[0], saved_grads[0],
     )
     grad_gate, grad_up = outer(late, d_gate, d_up)
-    return (next_acts[None], next_grads[None], grad_gate[None], grad_up[None])
+    return (next_acts[None], next_grads[None], grad_gate.T[None], grad_up.T[None])
 
 
 def solution(mesh):

time: 129 us -> 68.6 us (0.53); the launches traced: 127 us -> 68.3 us
  local copies, waits for them, and re-layouts: 61.6 us -> 2.94 us
    unnamed x10 -> x2, local copies, waits for them, and re-layouts: 61.6 us -> 2.94 us
where the time goes in v2:
time: 68.6 us; the launch traced here: 68.3 us
  Pallas kernels  64.7 us (94%)
  local copies, waits for them, and re-layouts  2.94 us (4%)
    pallas_call x1, Pallas kernels, body(): pl.pallas_call(tick_kernel, out_shape=(small, small, jax.ShapeDtypeStruct...  54.4 us
    pallas_call x1, Pallas kernels, outer(): pl.pallas_call(outer_kernel, grid=(width // STEP,), out_shape=(jax.ShapeD...  10.3 us
    unnamed x2, local copies, waits for them, and re-layouts  2.94 us

profile of v2, /device:TPU:0, one launch (start us, length us, event | category | flops | bytes accessed | tf_op | source)
XLA Modules:
  0.0 68.3 jit_solution(16353368113435167352)
XLA Ops:
  0.6 54.4 %shard_map.111 = (bf16[8,4096]{1,0:T(8,128)(2,1)}, bf16[8,4096]{1,0:T(8,128)(2,1)}, bf16[64,4096]{1,0:T(8,128)(2,1)}, bf16[64,1376]{1,0:T(8,128)(2,1)}, bf16[64,1376]{1,0:T(8,128)(2,1)}) custom-call(s32[1,2]{1,0:T(1,128)} %plan.1, bf16[1376,4096]{1,0:T(8,128)(2,1)} %bitcast.14, bf16[1376,4096]{1,0:T(8,128)(2,1)} %bitcast.15, bf16[1376,4096]{1,0:T(8,128)(2,1)} %w_down.1, ...), custom_call_target="tpu_custom_call" | custom-call | tf_op jit(solution)/shard_map/pallas_call | solution.py:441
  55.0 10.3 %shard_map.112 = (bf16[1376,4096]{1,0:T(8,128)(2,1)}, bf16[1376,4096]{1,0:T(8,128)(2,1)}) custom-call(bf16[64,4096]{1,0:T(8,128)(2,1)} %get-tuple-element.13.late, bf16[64,1376]{1,0:T(8,128)(2,1)} %get-tuple-element.14.d_gate, bf16[64,1376]{1,0:T(8,128)(2,1)} %get-tuple-element.15.d_up), custom_call_target="tpu_custom_call" | custom-call | flops 1442840576 | bytes 22544384 | tf_op jit(solution)/shard_map/pallas_call | solution.py:419
  65.3 1.5 %copy.14 = bf16[1,8,4096]{2,1,0:T(8,128)(2,1)} copy(bf16[1,8,4096]{2,1,0:T(8,128)(2,1)} %bitcast.21) | data formatting | bytes 131072
  66.8 1.5 %copy.15 = bf16[1,8,4096]{2,1,0:T(8,128)(2,1)} copy(bf16[1,8,4096]{2,1,0:T(8,128)(2,1)} %bitcast.20) | data formatting | bytes 131072

commit v3 on v2

--- a/solution.py
+++ b/solution.py
@@ -405,27 +405,31 @@
             block_copy(a, own_b, slot, partner).wait_send()
 
 
-def outer_kernel(late, d_gate, d_up, grad_gate, grad_up):
+def outer_kernel(late, d_gate, d_up, acts, grads, grad_gate, grad_up, next_acts, next_grads):
+    next_acts[...] = acts[...]
+    next_grads[...] = grads[...]
     right = late[...]
     grad_gate[...] = contract_rows(d_gate[...], right).astype(BF16)
     grad_up[...] = contract_rows(d_up[...], right).astype(BF16)
 
 
-def outer(late, d_gate, d_up):
+def outer(late, d_gate, d_up, acts, grads):
     tokens, width = late.shape
     hidden = d_gate.shape[1]
     whole = pl.BlockSpec((tokens, hidden), lambda i: (0, 0))
+    slim = pl.BlockSpec((acts.shape[0], STEP), lambda i: (0, i))
     tile = pl.BlockSpec((hidden, STEP), lambda i: (0, i))
     return pl.pallas_call(
         outer_kernel,
         grid=(width // STEP,),
-        out_shape=(jax.ShapeDtypeStruct((hidden, width), BF16),) * 2,
-        in_specs=[pl.BlockSpec((tokens, STEP), lambda i: (0, i)), whole, whole],
-        out_specs=(tile, tile),
+        out_shape=(jax.ShapeDtypeStruct((hidden, width), BF16),) * 2
+        + (jax.ShapeDtypeStruct(acts.shape, BF16),) * 2,
+        in_specs=[pl.BlockSpec((tokens, STEP), lambda i: (0, i)), whole, whole, slim, slim],
+        out_specs=(tile, tile, slim, slim),
         cost_estimate=pl.CostEstimate(
             flops=4 * tokens * width * hidden, bytes_accessed=4 * width * hidden, transcendentals=0
         ),
-    )(late, d_gate, d_up)
+    )(late, d_gate, d_up, acts, grads)
 
 
 def body(weight_gate, weight_up, weight_down, acts_in, grads_in, saved_acts, saved_grads, plan):
@@ -481,7 +485,7 @@
         plan, weight_gate.T, weight_up.T, weight_down,
         acts_in[0], grads_in[0], saved_acts[0], saved_grads[0],
     )
-    grad_gate, grad_up = outer(late, d_gate, d_up)
+    grad_gate, grad_up, next_acts, next_grads = outer(late, d_gate, d_up, next_acts, next_grads)
     return (next_acts[None], next_grads[None], grad_gate.T[None], grad_up.T[None])
 
 

time: 68.6 us -> 65.8 us (0.959)
  local copies, waits for them, and re-layouts: 2.94 us -> 0 us
    unnamed x2 -> x0, local copies, waits for them, and re-layouts: 2.94 us -> none
where the time goes in v3:
time: 65.8 us; the launch traced here: 65.4 us
  Pallas kernels  64.8 us (98%)
    pallas_call x1, Pallas kernels, body(): pl.pallas_call(tick_kernel, out_shape=(small, small, jax.ShapeDtypeStruct...  54.4 us
    pallas_call x1, Pallas kernels, outer(): pl.pallas_call(outer_kernel, grid=(width // STEP,), out_shape=(jax.ShapeD...  10.4 us

profile of v3, /device:TPU:0, one launch (start us, length us, event | category | flops | bytes accessed | tf_op | source)
XLA Modules:
  0.0 65.4 jit_solution(13512459045975497289)
XLA Ops:
  0.6 54.4 %shard_map.111 = (bf16[8,4096]{1,0:T(8,128)(2,1)}, bf16[8,4096]{1,0:T(8,128)(2,1)}, bf16[64,4096]{1,0:T(8,128)(2,1)}, bf16[64,1376]{1,0:T(8,128)(2,1)}, bf16[64,1376]{1,0:T(8,128)(2,1)}) custom-call(s32[1,2]{1,0:T(1,128)} %plan.1, bf16[1376,4096]{1,0:T(8,128)(2,1)} %bitcast.14, bf16[1376,4096]{1,0:T(8,128)(2,1)} %bitcast.15, bf16[1376,4096]{1,0:T(8,128)(2,1)} %w_down.1, ...), custom_call_target="tpu_custom_call" | custom-call | tf_op jit(solution)/shard_map/pallas_call | solution.py:445
  55.0 10.4 %shard_map.112 = (bf16[1376,4096]{1,0:T(8,128)(2,1)}, bf16[1376,4096]{1,0:T(8,128)(2,1)}, bf16[8,4096]{1,0:T(8,128)(2,1)}, bf16[8,4096]{1,0:T(8,128)(2,1)}) custom-call(bf16[64,4096]{1,0:T(8,128)(2,1)} %get-tuple-element.13.late, bf16[64,1376]{1,0:T(8,128)(2,1)} %get-tuple-element.14.d_gate, bf16[64,1376]{1,0:T(8,128)(2,1)} %get-tuple-element.15.d_up, ...), custom_call_target="tpu_custom_call" | custom-call | flops 1442840576 | bytes 22544384 | tf_op jit(solution)/shard_map/pallas_call | solution.py:422
